TPU v7x, 32 devices: a whole 2x2x4 slice. The times are simulated.
32 devices in a mesh: section: 2 (over core), ctx: 8 (over z, x), dp: 2 (over y).
Axes of the slice: x: 2, y: 2, z: 4, core: 2. Of those that a mesh axis runs over, the one named last changes fastest.
Arguments:
- hidden: bfloat16 [4, 2048, 5376], P(('section', 'dp'), 'ctx'), may hold values from -6 to 6
- frozen_query_rows: bfloat16 [4, 2048, 2048], P(('section', 'dp'), 'ctx'), may hold values from -12 to 12
- frozen_key_rows: bfloat16 [4, 2048, 1024], P(('section', 'dp'), 'ctx'), may hold values from -12 to 12
- frozen_value_rows: bfloat16 [4, 2048, 1024], P(('section', 'dp'), 'ctx'), may hold values from -6 to 6
- next_output_gradient: bfloat16 [4, 2048, 2048], P(('section', 'dp'), 'ctx'), may hold values from -0.011962891 to 0.011962891
- document_lengths: int32 [4, 16], P(('section', 'dp')), may hold values from 1 to 512, 2048 in all within a row
- document_adapter: int32 [4, 16], P(('section', 'dp')), may hold values from 0 to 3
- adapter_down_maps: bfloat16 [5376, 2, 4, 16], replicated, may hold values from -0.078125 to 0.078125
- adapter_up_maps: bfloat16 [2, 4, 16, 1024], replicated, may hold values from -1.5 to 1.5
Outputs:
- handed_on: bfloat16 [4, 2048, 2048], P(('section', 'dp'), 'ctx')
- down_map_gradient: float32 [5376, 2, 4, 16], replicated
- up_map_gradient: float32 [2, 4, 16, 1024], replicated
Inputs may be any that keep to these rules, and one draw needn't show every extreme that they name: `document_lengths`: each sequence's 16 lengths sum to 2048, and the longest is exactly 512.
All inputs are finite; a program needn't handle non-finite values.
Results may differ from a plain program's by a relative error of at most 0.016.
Values may be sent and summed in bfloat16 or wider, within the bound.
No kernel may reach another device: no remote copies, remote signals or barrier semaphores. Data moves between devices by JAX's collectives and lax.ppermute only.
A program may use at most 128 MiB of HBM per device.

v0:
```python
from functools import partial
import jax
import jax.numpy as jnp
from jax import lax
from jax.sharding import PartitionSpec as P

HD = 128
WINDOW = 1024
query_scale = 168.0 ** (-0.5)
adapter_scale = 0.5
rope_base = 10000.0
masked_score = -1e30


def passed_along(value, axis, by):
    length = lax.axis_size(axis)
    return lax.ppermute(value, axis, [(i, (i + by) % length) for i in range(length)])


def passed_along_2(value, axis, steps):
    count = lax.axis_size(axis)
    initial, last = (max(0, -steps), min(count, count - steps))
    return lax.ppermute(value, axis, [(source, source + steps) for source in range(initial, last)])


def rotate(vectors, positions, direction):
    head_dim = vectors.shape[-1]
    half_dim = head_dim // 2
    frequency = rope_base ** (-(jnp.arange(half_dim, dtype=jnp.float32) * 2.0) / head_dim)
    angles = positions[:, None] * frequency[None, :]
    cos_part = jnp.cos(angles)[:, None, :]
    sine_part = direction * jnp.sin(angles)[:, None, :]
    front_half = vectors[..., :half_dim]
    back_half = vectors[..., half_dim:]
    return jnp.concatenate(
        [
            front_half * cos_part - back_half * sine_part,
            back_half * cos_part + front_half * sine_part,
        ],
        axis=-1,
    )


def doc_index(sequence_lengths, positions):
    doc_ends = jnp.cumsum(sequence_lengths)
    return jnp.sum((doc_ends[None, :] <= positions[:, None]).astype(jnp.int32), axis=1)


def tenant_rows(sequence_lengths, adapter_bank, positions):
    doc_ids = doc_index(sequence_lengths, positions)
    picked = (
        doc_ids[:, None] == jnp.arange(sequence_lengths.shape[0], dtype=jnp.int32)[None, :]
    ).astype(jnp.int32)
    return (doc_ids, jnp.sum(picked * adapter_bank[None, :], axis=1))


def adapter_token_rows(
    hidden, frozen_key_rows, frozen_value_rows, adapter_down_maps, adapter_up_maps, adapter_choice
):
    token_row_count = hidden.shape[0]
    adapter_choices = adapter_up_maps.shape[1]
    adapter_rank_size = adapter_up_maps.shape[2]
    key_value_width = adapter_up_maps.shape[3]
    adapter_onehot_mask = (
        adapter_choice[:, None] == jnp.arange(adapter_choices, dtype=jnp.int32)[None, :]
    ).astype(jnp.float32)
    low_rank_rows = jnp.dot(
        hidden,
        adapter_down_maps.reshape(
            adapter_down_maps.shape[0], 2 * adapter_choices * adapter_rank_size
        ),
        preferred_element_type=jnp.float32,
    )
    low_rank_rows = low_rank_rows.reshape(token_row_count, 2, adapter_choices, adapter_rank_size)
    low_rank = jnp.sum(low_rank_rows * adapter_onehot_mask[:, None, :, None], axis=2).astype(
        jnp.bfloat16
    )
    adapter_spread = low_rank[:, :, None, :] * adapter_onehot_mask[:, None, :, None].astype(
        jnp.bfloat16
    )
    key_adapter_shift = jnp.dot(
        adapter_spread[:, 0].reshape(token_row_count, adapter_choices * adapter_rank_size),
        adapter_up_maps[0].reshape(adapter_choices * adapter_rank_size, key_value_width),
        preferred_element_type=jnp.float32,
    )
    value_adapter_shift = jnp.dot(
        adapter_spread[:, 1].reshape(token_row_count, adapter_choices * adapter_rank_size),
        adapter_up_maps[1].reshape(adapter_choices * adapter_rank_size, key_value_width),
        preferred_element_type=jnp.float32,
    )
    key_before_rotary = frozen_key_rows.astype(jnp.float32) + adapter_scale * key_adapter_shift
    value_token_rows = (
        frozen_value_rows.astype(jnp.float32) + adapter_scale * value_adapter_shift
    ).astype(jnp.bfloat16)
    return (adapter_onehot_mask, adapter_spread, key_before_rotary, value_token_rows)


def adapter_gradients(
    hidden, adapter_spread, adapter_onehot_mask, key_gradient, value_gradient, adapter_up_maps
):
    token_row_count = hidden.shape[0]
    adapter_choices = adapter_up_maps.shape[1]
    adapter_rank_size = adapter_up_maps.shape[2]
    key_value_width = adapter_up_maps.shape[3]
    up_gradient_parts = []
    down_parts = []
    for adapter_selector, adapter_field_gradient in ((0, key_gradient), (1, value_gradient)):
        flat_adapter_spread = adapter_spread[:, adapter_selector].reshape(
            token_row_count, adapter_choices * adapter_rank_size
        )
        up_gradient_parts.append(
            adapter_scale
            * jnp.dot(
                flat_adapter_spread.T, adapter_field_gradient, preferred_element_type=jnp.float32
            )
        )
        low_rank_gradient = adapter_scale * jnp.dot(
            adapter_field_gradient,
            adapter_up_maps[adapter_selector]
            .reshape(adapter_choices * adapter_rank_size, key_value_width)
            .T,
            preferred_element_type=jnp.float32,
        )
        down_parts.append(
            (
                low_rank_gradient.reshape(token_row_count, adapter_choices, adapter_rank_size)
                * adapter_onehot_mask[:, :, None]
            ).astype(jnp.bfloat16)
        )
    up_map_gradient = jnp.stack(up_gradient_parts).reshape(
        2, adapter_choices, adapter_rank_size, key_value_width
    )
    low_grads = jnp.stack(down_parts, axis=1).reshape(
        token_row_count, 2 * adapter_choices * adapter_rank_size
    )
    down_map_gradient = jnp.dot(hidden.T, low_grads, preferred_element_type=jnp.float32).reshape(
        hidden.shape[1], 2, adapter_choices, adapter_rank_size
    )
    return (down_map_gradient, up_map_gradient)


def masked_scores(query_part, key_part, allowed):
    scores = (
        jnp.einsum("trd,ld->trl", query_part, key_part, preferred_element_type=jnp.float32)
        * query_scale
    )
    return jnp.where(allowed[:, None, :], scores, masked_score)


def group_forward(operands, allowed):
    query_part, key_part, value_part = operands
    scores = masked_scores(query_part, key_part, allowed)
    row_max = jnp.max(scores, axis=2, keepdims=True)
    shifted = jnp.exp(scores - row_max)
    row_total = jnp.sum(shifted, axis=2, keepdims=True)
    weights = (shifted / row_total).astype(jnp.bfloat16)
    output_rows = jnp.einsum(
        "trl,ld->trd", weights, value_part, preferred_element_type=jnp.float32
    ).astype(jnp.bfloat16)
    return (output_rows, (row_max + jnp.log(row_total))[..., 0])


def group_backward(operands, allowed):
    query_part, key_part, value_part, out_part, grad_part, log_total = operands
    scores = masked_scores(query_part, key_part, allowed)
    weights = jnp.exp(scores - log_total[:, :, None])
    weights_low = weights.astype(jnp.bfloat16)
    drift_rows = jnp.sum(grad_part.astype(jnp.float32) * out_part.astype(jnp.float32), axis=2)
    grad_weights = jnp.einsum(
        "trd,ld->trl", grad_part, value_part, preferred_element_type=jnp.float32
    )
    grad_scores = (weights * (grad_weights - drift_rows[:, :, None])).astype(jnp.bfloat16)
    value_step = jnp.einsum(
        "trl,trd->ld", weights_low, grad_part, preferred_element_type=jnp.float32
    )
    key_step = (
        jnp.einsum("trl,trd->ld", grad_scores, query_part, preferred_element_type=jnp.float32)
        * query_scale
    )
    return (key_step, value_step)


def body(
    hidden,
    frozen_query_rows,
    frozen_key_rows,
    frozen_value_rows,
    next_output_gradient,
    document_lengths,
    document_adapter,
    adapter_down_maps,
    adapter_up_maps,
):
    tok_rows = hidden.shape[1]
    query_width = frozen_query_rows.shape[2]
    key_value_width = frozen_key_rows.shape[2]
    kv_heads = key_value_width // HD
    group_size = query_width // key_value_width
    ctx_index = lax.axis_index("ctx")
    reach_devs = min(WINDOW // tok_rows, lax.axis_size("ctx") - 1)
    returned_values = passed_along(next_output_gradient, "section", -1)
    positions = ctx_index * tok_rows + jnp.arange(tok_rows, dtype=jnp.int32)
    doc_ids, adapter_choice = tenant_rows(document_lengths[0], document_adapter[0], positions)
    adapter_onehot_mask, adapter_spread, key_before_rotary, value_token_rows = adapter_token_rows(
        hidden[0],
        frozen_key_rows[0],
        frozen_value_rows[0],
        adapter_down_maps,
        adapter_up_maps,
        adapter_choice,
    )
    pos_float = positions.astype(jnp.float32)
    key_rows = (
        rotate(key_before_rotary.reshape(tok_rows, kv_heads, HD), pos_float, 1.0)
        .astype(jnp.bfloat16)
        .reshape(tok_rows, key_value_width)
    )
    query_rows = rotate(
        frozen_query_rows[0].astype(jnp.float32).reshape(tok_rows, kv_heads * group_size, HD),
        pos_float,
        1.0,
    ).astype(jnp.bfloat16)
    received = []
    moving = (key_rows, value_token_rows)
    for distance in range(reach_devs):
        moving = passed_along_2((moving[0], moving[1]), "ctx", 1)
        received.append(moving)
    far_first = received[::-1]
    key_all = jnp.concatenate([kv_pair[0] for kv_pair in far_first] + [key_rows], axis=0)
    value_all = jnp.concatenate([kv_pair[1] for kv_pair in far_first] + [value_token_rows], axis=0)
    key_pos = (ctx_index - reach_devs) * tok_rows + jnp.arange(
        (reach_devs + 1) * tok_rows, dtype=jnp.int32
    )
    key_docs = doc_index(document_lengths[0], key_pos)
    key_gap = positions[:, None] - key_pos[None, :]
    allowed = (
        (doc_ids[:, None] == key_docs[None, :])
        & (key_gap >= 0)
        & (key_gap < WINDOW)
        & (key_pos >= 0)[None, :]
    )
    query_groups = jnp.moveaxis(query_rows.reshape(tok_rows, kv_heads, group_size, HD), 1, 0)
    key_groups = jnp.moveaxis(key_all.reshape(-1, kv_heads, HD), 1, 0)
    value_groups = jnp.moveaxis(value_all.reshape(-1, kv_heads, HD), 1, 0)
    out_groups, log_groups = lax.map(
        partial(group_forward, allowed=allowed), (query_groups, key_groups, value_groups)
    )
    attention_output = jnp.moveaxis(out_groups, 0, 1).reshape(1, tok_rows, query_width)
    handed = passed_along(attention_output, "section", 1)
    grad_groups = jnp.moveaxis(returned_values[0].reshape(tok_rows, kv_heads, group_size, HD), 1, 0)
    key_grads, value_grads = lax.map(
        partial(group_backward, allowed=allowed),
        (query_groups, key_groups, value_groups, out_groups, grad_groups, log_groups),
    )
    key_grads = jnp.moveaxis(key_grads, 0, 1).reshape(-1, key_value_width)
    value_grads = jnp.moveaxis(value_grads, 0, 1).reshape(-1, key_value_width)

    def rows_at(field_rows, distance):
        return field_rows[
            (reach_devs - distance) * tok_rows : (reach_devs - distance + 1) * tok_rows
        ]

    carried = (rows_at(key_grads, reach_devs), rows_at(value_grads, reach_devs))
    for distance in range(reach_devs - 1, -1, -1):
        carried = passed_along_2((carried[0], carried[1]), "ctx", -1)
        carried = (
            carried[0] + rows_at(key_grads, distance),
            carried[1] + rows_at(value_grads, distance),
        )
    key_back, value_back = carried
    key_gradient = (
        rotate(key_back.reshape(tok_rows, kv_heads, HD), pos_float, -1.0)
        .astype(jnp.bfloat16)
        .reshape(tok_rows, key_value_width)
    )
    value_gradient = value_back.astype(jnp.bfloat16)
    down_map_gradient, up_map_gradient = adapter_gradients(
        hidden[0],
        adapter_spread,
        adapter_onehot_mask,
        key_gradient,
        value_gradient,
        adapter_up_maps,
    )
    summed = lax.psum((down_map_gradient, up_map_gradient), ("section", "ctx", "dp"))
    return (handed, summed[0], summed[1])


def solution(mesh):
    return jax.shard_map(
        body,
        mesh=mesh,
        in_specs=(
            P(("section", "dp"), "ctx", None),
            P(("section", "dp"), "ctx", None),
            P(("section", "dp"), "ctx", None),
            P(("section", "dp"), "ctx", None),
            P(("section", "dp"), "ctx", None),
            P(("section", "dp"), None),
            P(("section", "dp"), None),
            P(),
            P(),
        ),
        out_specs=(P(("section", "dp"), "ctx", None), P(), P()),
        check_vma=False,
    )
```

profile of v0, /device:TPU:0, one launch (start us, length us, event | category | flops | bytes accessed | tf_op | source)
XLA Modules:
  0.0 638.7 jit_solution(13565225289575519029)
XLA Ops:
  17.9 5.7 collective-permute-start
  24.7 3.5 collective-permute-start.4
  28.1 6.9 %collective-permute-done = bf16[256,1024]{0,1:T(8,128)(2,1)} collective-permute-done((bf16[256,1024]{0,1:T(8,128)(2,1)S(1)}, bf16[256,1024]{0,1:T(8,128)(2,1)}, u32[]{:S(2)}, u32[]{:S(2)}) %collective-permute-start) | collective-permute-done | bytes 524320 | tf_op jit(solution)/shard_map/ppermute | solution.py:23
  35.0 5.3 collective-permute-start.1
  46.4 5.2 collective-permute-start.5
  51.5 6.1 collective-permute-done.1
  57.6 5.2 collective-permute-start.2
  68.8 5.2 collective-permute-start.6
  74.0 6.0 collective-permute-done.2
  80.1 4.4 collective-permute-start.3
  87.5 3.8 collective-permute-done.6
  91.3 5.2 collective-permute-start.7
  96.5 6.1 collective-permute-done.3
  109.8 4.4 copy.48
  121.6 46.0 %while.26 = (s32[]{:T(128)}, bf16[8,256,2,128]{3,1,2,0:T(8,128)(2,1)}, f32[8,256,2]{1,2,0:T(2,128)}, bf16[8,256,2,128]{3,1,2,0:T(8,128)(2,1)}, bf16[8,1280,128]{...) while((s32[]{:T(128)}, ...), condition=%wide.region_8.9_spmd.clone, body=%wide.region_5.8_spmd.clone.sunk | while | flops 343145984 | bytes 9469813 | solution.py:245
  167.7 127.0 %while.27 = (s32[]{:T(128)}, f32[8,1280,128]{1,2,0:T(8,128)}, f32[8,1280,128]{1,2,0:T(8,128)}, bf16[8,256,2,128]{3,1,2,0:T(8,128)(2,1)}, bf16[8,1280,128]{2,1,0:...) while((s32[]{:T(128)}, f32[8,1280,128]{1,2,0:T(8,128)}, ...), condition=%wide.region_11.12_spmd.clone, body=%wide.region_9.11_spmd.clone.sunk | while | flops 678395392 | bytes 14472769 | solution.py:251
  168.9 3.3 fusion.128
  174.3 3.9 fusion.130
  184.8 3.3 fusion.128
  190.2 3.9 fusion.130
  200.6 3.3 fusion.128
  206.1 3.9 fusion.130
  212.2 3.1 fusion.131
  216.6 3.3 fusion.128
  222.0 3.9 fusion.130
  228.1 3.1 fusion.131
  232.5 3.3 fusion.128
  238.0 3.9 fusion.130
  244.1 3.0 fusion.131
  248.3 3.3 fusion.128
  253.8 3.9 fusion.130
  259.9 3.0 fusion.131
  264.2 3.3 fusion.128
  269.7 3.9 fusion.130
  280.1 3.3 fusion.128
  285.5 3.9 fusion.130
  301.2 24.9 %collective-permute-done.14 = f32[256,1024]{0,1:T(8,128)S(1)} collective-permute-done((f32[256,1024]{0,1:T(8,128)S(1)}, f32[256,1024]{0,1:T(8,128)S(1)}, u32[]{:S(2)}, u32[]{:S(2)}) %collective-permute-start.14) | collective-permute-done | bytes 1048608 | tf_op jit(solution)/shard_map/ppermute | solution.py:23
  327.6 21.0 %collective-permute-done.10 = f32[256,1024]{0,1:T(8,128)S(1)} collective-permute-done((f32[256,1024]{0,1:T(8,128)S(1)}, f32[256,1024]{0,1:T(8,128)S(1)}, u32[]{:S(2)}, u32[]{:S(2)}) %collective-permute-start.10) | collective-permute-done | bytes 1048608 | tf_op jit(solution)/shard_map/ppermute | solution.py:23
  350.1 21.0 %collective-permute-done.15 = f32[256,1024]{0,1:T(8,128)S(1)} collective-permute-done((f32[256,1024]{0,1:T(8,128)S(1)}, f32[256,1024]{0,1:T(8,128)S(1)}, u32[]{:S(2)}, u32[]{:S(2)}) %collective-permute-start.15) | collective-permute-done | bytes 1048608 | tf_op jit(solution)/shard_map/ppermute | solution.py:23
  372.6 21.0 %collective-permute-done.11 = f32[256,1024]{0,1:T(8,128)S(1)} collective-permute-done((f32[256,1024]{0,1:T(8,128)S(1)}, f32[256,1024]{0,1:T(8,128)S(1)}, u32[]{:S(2)}, u32[]{:S(2)}) %collective-permute-start.11) | collective-permute-done | bytes 1048608 | tf_op jit(solution)/shard_map/ppermute | solution.py:23
  395.0 21.0 %collective-permute-done.16 = f32[256,1024]{0,1:T(8,128)S(1)} collective-permute-done((f32[256,1024]{0,1:T(8,128)S(1)}, f32[256,1024]{0,1:T(8,128)S(1)}, u32[]{:S(2)}, u32[]{:S(2)}) %collective-permute-start.16) | collective-permute-done | bytes 1048608 | tf_op jit(solution)/shard_map/ppermute | solution.py:23
  417.5 21.0 %collective-permute-done.12 = f32[256,1024]{0,1:T(8,128)S(1)} collective-permute-done((f32[256,1024]{0,1:T(8,128)S(1)}, f32[256,1024]{0,1:T(8,128)S(1)}, u32[]{:S(2)}, u32[]{:S(2)}) %collective-permute-start.12) | collective-permute-done | bytes 1048608 | tf_op jit(solution)/shard_map/ppermute | solution.py:23
  440.3 20.8 %collective-permute-done.17 = f32[256,1024]{0,1:T(8,128)S(1)} collective-permute-done((f32[256,1024]{0,1:T(8,128)S(1)}, f32[256,1024]{0,1:T(8,128)S(1)}, u32[]{:S(2)}, u32[]{:S(2)}) %collective-permute-start.17) | collective-permute-done | bytes 1048608 | tf_op jit(solution)/shard_map/ppermute | solution.py:23
  461.7 18.9 %collective-permute-done.13 = f32[256,1024]{0,1:T(8,128)S(1)} collective-permute-done((f32[256,1024]{0,1:T(8,128)S(1)}, f32[256,1024]{0,1:T(8,128)S(1)}, u32[]{:S(2)}, u32[]{:S(2)}) %collective-permute-start.13) | collective-permute-done | bytes 1048608 | tf_op jit(solution)/shard_map/ppermute | solution.py:23
  484.5 3.3 copy.49
  490.4 3.3 collective-permute-done.8
  493.7 131.4 %all-reduce.3.cloned.1.call-done = (f32[5376,2,4,16]{0,3,2,1:T(8,128)}, f32[2,4,16,1024]{3,2,1,0:T(8,128)}) async-done(((f32[5376,2,4,16]{0,3,2,1:T(8,128)}, f32[2,4,16,1024]{3,2,1,0:T(8,128)}), (f32[5376,2,4,16]{0,3,2,1:T(8,128)}, f32[2,4,16,1024]{3,2,1,0:T(8,128)})) %all-reduce.3.cloned.1.call-update) | async-done | bytes 3276816 | tf_op jit(solution)/shard_map/psum | solution.py:285
  627.5 3.6 copy.114
  (319 shorter events, 169.1 us)
Async XLA Ops:
  7.2 618.0 %all-reduce.3.cloned.1.call-start = ((), (), s32[]{:S(2)}) async-start(), calls=%async_computation | async-start | bytes 6553600 | tf_op jit(solution)/shard_map/psum | solution.py:285
  15.5 8.0 %copy-start.5 = (bf16[2,4,16,1024]{3,2,1,0:T(8,128)(2,1)S(1)}, bf16[2,4,16,1024]{3,2,1,0:T(8,128)(2,1)}, u32[]{:S(2)}) copy-start(bf16[2,4,16,1024]{3,2,1,0:T(8,128)(2,1)} %param.21) | copy-start | bytes 786436
  15.5 8.0 %copy-start.22 = (bf16[1,256,1024]{2,1,0:T(8,128)(2,1)S(1)}, bf16[1,256,1024]{2,1,0:T(8,128)(2,1)}, u32[]{:S(2)}) copy-start(bf16[1,256,1024]{2,1,0:T(8,128)(2,1)} %param.16) | copy-start | bytes 1572868
  17.9 17.2 %collective-permute-start = (bf16[256,1024]{0,1:T(8,128)(2,1)S(1)}, bf16[256,1024]{0,1:T(8,128)(2,1)}, u32[]{:S(2)}, u32[]{:S(2)}) collective-permute-start(bf16[256,1024]{0,1:T(8,128)(2,1)S(1)} %bitcast.243), channel_id=1, source_target_pairs={{0,2},{2,4},{4,6},{6,8},{8,10},{10,12},{12,14},{1,3},{3,5},{5,7},{... | collective-permute-start | bytes 1572872 | tf_op jit(solution)/shard_map/ppermute | solution.py:23
  24.7 21.7 %collective-permute-start.4 = (bf16[256,1024]{1,0:T(8,128)(2,1)}, bf16[256,1024]{1,0:T(8,128)(2,1)}, u32[]{:S(2)}, u32[]{:S(2)}) collective-permute-start(bf16[256,1024]{1,0:T(8,128)(2,1)} %fusion.59), channel_id=1, source_target_pairs={{0,2},{2,4},{4,6},{6,8},{8,10},{10,12},{12,14},{1,3},{3,5},{5,7},{... | collective-permute-start | bytes 1572872 | tf_op jit(solution)/shard_map/ppermute | solution.py:23
  35.0 22.6 %collective-permute-start.1 = (bf16[256,1024]{0,1:T(8,128)(2,1)}, bf16[256,1024]{0,1:T(8,128)(2,1)}, u32[]{:S(2)}, u32[]{:S(2)}) collective-permute-start(bf16[256,1024]{0,1:T(8,128)(2,1)} %collective-permute-done), channel_id=1, source_target_pairs={{0,2},{2,4},{4,6},{6,8},{8,10},{10,12},{12,14},{1,3},{3,5},{5,7},{... | collective-permute-start | bytes 1572872 | tf_op jit(solution)/shard_map/ppermute | solution.py:23
  42.6 125.1 %collective-permute-start.9 = (bf16[1,256,2048]{1,2,0:T(8,128)(2,1)}, bf16[1,256,2048]{1,2,0:T(8,128)(2,1)}, u32[]{:S(2)}, u32[]{:S(2)}) collective-permute-start(bf16[1,256,2048]{1,2,0:T(8,128)(2,1)} %copy.50), channel_id=1, source_target_pairs={{0,16},{16,0},{1,17},{17,1},{2,18},{18,2},{3,19},{19,3},{4,20},{20... | collective-permute-start | bytes 3145736 | tf_op jit(solution)/shard_map/ppermute | solution.py:17
  46.4 22.5 %collective-permute-start.5 = (bf16[256,1024]{1,0:T(8,128)(2,1)}, bf16[256,1024]{1,0:T(8,128)(2,1)}, u32[]{:S(2)}, u32[]{:S(2)}) collective-permute-start(bf16[256,1024]{1,0:T(8,128)(2,1)} %collective-permute-done.4), channel_id=1, source_target_pairs={{0,2},{2,4},{4,6},{6,8},{8,10},{10,12},{12,14},{1,3},{3,5},{5,7},{... | collective-permute-start | bytes 1572872 | tf_op jit(solution)/shard_map/ppermute | solution.py:23
  57.6 22.5 %collective-permute-start.2 = (bf16[256,1024]{0,1:T(8,128)(2,1)}, bf16[256,1024]{0,1:T(8,128)(2,1)}, u32[]{:S(2)}, u32[]{:S(2)}) collective-permute-start(bf16[256,1024]{0,1:T(8,128)(2,1)} %collective-permute-done.1), channel_id=1, source_target_pairs={{0,2},{2,4},{4,6},{6,8},{8,10},{10,12},{12,14},{1,3},{3,5},{5,7},{... | collective-permute-start | bytes 1572872 | tf_op jit(solution)/shard_map/ppermute | solution.py:23
  66.9 17.6 %copy-start.1 = (f32[256,64]{1,0:T(8,128)S(1)}, f32[256,64]{1,0:T(8,128)}, u32[]{:S(2)}) copy-start(f32[256,64]{1,0:T(8,128)} %copy.41) | copy-start | bytes 196612
  66.9 17.6 %copy-start.2 = (f32[256,64]{1,0:T(8,128)S(1)}, f32[256,64]{1,0:T(8,128)}, u32[]{:S(2)}) copy-start(f32[256,64]{1,0:T(8,128)} %copy.43) | copy-start | bytes 196612
  68.8 22.5 %collective-permute-start.6 = (bf16[256,1024]{1,0:T(8,128)(2,1)}, bf16[256,1024]{1,0:T(8,128)(2,1)}, u32[]{:S(2)}, u32[]{:S(2)}) collective-permute-start(bf16[256,1024]{1,0:T(8,128)(2,1)} %collective-permute-done.5), channel_id=1, source_target_pairs={{0,2},{2,4},{4,6},{6,8},{8,10},{10,12},{12,14},{1,3},{3,5},{5,7},{... | collective-permute-start | bytes 1572872 | tf_op jit(solution)/shard_map/ppermute | solution.py:23
  80.1 22.5 %collective-permute-start.3 = (bf16[256,1024]{0,1:T(8,128)(2,1)}, bf16[256,1024]{0,1:T(8,128)(2,1)S(1)}, u32[]{:S(2)}, u32[]{:S(2)}) collective-permute-start(bf16[256,1024]{0,1:T(8,128)(2,1)} %collective-permute-done.2), channel_id=1, source_target_pairs={{0,2},{2,4},{4,6},{6,8},{8,10},{10,12},{12,14},{1,3},{3,5},{5,7},{... | collective-permute-start | bytes 1572872 | tf_op jit(solution)/shard_map/ppermute | solution.py:23
  91.3 22.9 %collective-permute-start.7 = (bf16[256,1024]{1,0:T(8,128)(2,1)}, bf16[256,1024]{1,0:T(8,128)(2,1)}, u32[]{:S(2)}, u32[]{:S(2)}) collective-permute-start(bf16[256,1024]{1,0:T(8,128)(2,1)} %collective-permute-done.6), channel_id=1, source_target_pairs={{0,2},{2,4},{4,6},{6,8},{8,10},{10,12},{12,14},{1,3},{3,5},{5,7},{... | collective-permute-start | bytes 1572872 | tf_op jit(solution)/shard_map/ppermute | solution.py:23
  167.7 4.5 copy-start.9
  167.7 4.5 copy-start.13
  167.7 4.5 copy-start.17
  183.5 4.6 copy-start.9
  183.5 4.6 copy-start.13
  183.5 4.6 copy-start.17
  199.4 4.6 copy-start.9
  199.4 4.6 copy-start.13
  199.4 4.5 copy-start.17
  215.3 4.6 copy-start.9
  215.3 4.6 copy-start.13
  215.3 4.6 copy-start.17
  231.2 4.6 copy-start.9
  231.3 4.6 copy-start.13
  231.3 4.6 copy-start.17
  247.1 4.6 copy-start.9
  247.1 4.5 copy-start.13
  263.0 4.6 copy-start.9
  263.0 4.6 copy-start.13
  263.0 4.6 copy-start.17
  278.9 4.6 copy-start.9
  278.9 4.6 copy-start.13
  278.9 4.5 copy-start.17
  297.8 28.4 %collective-permute-start.14 = (f32[256,1024]{0,1:T(8,128)S(1)}, f32[256,1024]{0,1:T(8,128)S(1)}, u32[]{:S(2)}, u32[]{:S(2)}) collective-permute-start(f32[256,1024]{0,1:T(8,128)S(1)} %bitcast.238), channel_id=1, source_target_pairs={{2,0},{4,2},{6,4},{8,6},{10,8},{12,10},{14,12},{3,1},{5,3},{7,5},{... | collective-permute-start | bytes 3145736 | tf_op jit(solution)/shard_map/ppermute | solution.py:23
  299.9 48.7 %collective-permute-start.10 = (f32[256,1024]{0,1:T(8,128)S(1)}, f32[256,1024]{0,1:T(8,128)S(1)}, u32[]{:S(2)}, u32[]{:S(2)}) collective-permute-start(f32[256,1024]{0,1:T(8,128)S(1)} %bitcast.239), channel_id=1, source_target_pairs={{2,0},{4,2},{6,4},{8,6},{10,8},{12,10},{14,12},{3,1},{5,3},{7,5},{... | collective-permute-start | bytes 3145736 | tf_op jit(solution)/shard_map/ppermute | solution.py:23
  326.3 44.8 %collective-permute-start.15 = (f32[256,1024]{0,1:T(8,128)S(1)}, f32[256,1024]{0,1:T(8,128)S(1)}, u32[]{:S(2)}, u32[]{:S(2)}) collective-permute-start(f32[256,1024]{0,1:T(8,128)S(1)} %bitcast_add_fusion.3), channel_id=1, source_target_pairs={{2,0},{4,2},{6,4},{8,6},{10,8},{12,10},{14,12},{3,1},{5,3},{7,5},{... | collective-permute-start | bytes 3145736 | tf_op jit(solution)/shard_map/ppermute | solution.py:23
  348.8 44.8 %collective-permute-start.11 = (f32[256,1024]{0,1:T(8,128)S(1)}, f32[256,1024]{0,1:T(8,128)S(1)}, u32[]{:S(2)}, u32[]{:S(2)}) collective-permute-start(f32[256,1024]{0,1:T(8,128)S(1)} %bitcast_add_fusion.7), channel_id=1, source_target_pairs={{2,0},{4,2},{6,4},{8,6},{10,8},{12,10},{14,12},{3,1},{5,3},{7,5},{... | collective-permute-start | bytes 3145736 | tf_op jit(solution)/shard_map/ppermute | solution.py:23
  371.3 44.8 %collective-permute-start.16 = (f32[256,1024]{0,1:T(8,128)S(1)}, f32[256,1024]{0,1:T(8,128)S(1)}, u32[]{:S(2)}, u32[]{:S(2)}) collective-permute-start(f32[256,1024]{0,1:T(8,128)S(1)} %bitcast_add_fusion.2), channel_id=1, source_target_pairs={{2,0},{4,2},{6,4},{8,6},{10,8},{12,10},{14,12},{3,1},{5,3},{7,5},{... | collective-permute-start | bytes 3145736 | tf_op jit(solution)/shard_map/ppermute | solution.py:23
  393.7 44.8 %collective-permute-start.12 = (f32[256,1024]{0,1:T(8,128)S(1)}, f32[256,1024]{0,1:T(8,128)S(1)}, u32[]{:S(2)}, u32[]{:S(2)}) collective-permute-start(f32[256,1024]{0,1:T(8,128)S(1)} %bitcast_add_fusion.6), channel_id=1, source_target_pairs={{2,0},{4,2},{6,4},{8,6},{10,8},{12,10},{14,12},{3,1},{5,3},{7,5},{... | collective-permute-start | bytes 3145736 | tf_op jit(solution)/shard_map/ppermute | solution.py:23
  416.1 24.1 %copy-start.6 = (bf16[2,4,16,1024]{3,2,1,0:T(8,128)(2,1)S(1)}, bf16[2,4,16,1024]{3,2,1,0:T(8,128)(2,1)}, u32[]{:S(2)}) copy-start(bf16[2,4,16,1024]{3,2,1,0:T(8,128)(2,1)} %param.21) | copy-start | bytes 786436
  416.2 44.8 %collective-permute-start.17 = (f32[256,1024]{0,1:T(8,128)S(1)}, f32[256,1024]{0,1:T(8,128)S(1)}, u32[]{:S(2)}, u32[]{:S(2)}) collective-permute-start(f32[256,1024]{0,1:T(8,128)S(1)} %bitcast_add_fusion.1), channel_id=1, source_target_pairs={{2,0},{4,2},{6,4},{8,6},{10,8},{12,10},{14,12},{3,1},{5,3},{7,5},{... | collective-permute-start | bytes 3145736 | tf_op jit(solution)/shard_map/ppermute | solution.py:23
  438.7 42.0 %collective-permute-start.13 = (f32[256,1024]{0,1:T(8,128)S(1)}, f32[256,1024]{0,1:T(8,128)S(1)}, u32[]{:S(2)}, u32[]{:S(2)}) collective-permute-start(f32[256,1024]{0,1:T(8,128)S(1)} %bitcast_add_fusion.5), channel_id=1, source_target_pairs={{2,0},{4,2},{6,4},{8,6},{10,8},{12,10},{14,12},{3,1},{5,3},{7,5},{... | collective-permute-start | bytes 3145736 | tf_op jit(solution)/shard_map/ppermute | solution.py:23
  461.2 19.6 %copy-start.7 = (f32[256,64]{0,1:T(8,128)S(1)}, f32[256,64]{0,1:T(8,128)}, u32[]{:S(2)}) copy-start(f32[256,64]{0,1:T(8,128)} %get-tuple-element.290) | copy-start | bytes 196612
  490.4 3.3 collective-permute-start.8
  (38 other events, 111.6 us)
Sparse Core Ops, SparseCore 0:
  484.6 140.5 all-reduce.2
where the time goes:
time: 642 us; the launch traced here: 639 us
  waiting for transfers between devices  336 us (52%)
  matrix products  123 us (19%)
  local copies, waits for them, and re-layouts  75.9 us (12%)
  starting transfers between devices  50.3 us (8%)
  other arithmetic  39.1 us (6%)
  between operations  14.5 us (2%)
    ppermute x16, waiting for transfers between devices, passed_along_2(): lax.ppermute(value, axis, [(source, source + steps) for source in range(i...  201 us
    psum x1, waiting for transfers between devices, body(): lax.psum((down_map_gradient, up_map_gradient), ('section', 'ctx', 'dp'))  131 us
    ppermute x16, starting transfers between devices, passed_along_2(): lax.ppermute(value, axis, [(source, source + steps) for source in range(i...  50.3 us
    dot_general x16, matrix products, masked_scores(): jnp.einsum('trd,ld->trl', query_part, key_part, preferred_element_type=jn...  40.9 us
    dot_general x8, matrix products, group_backward(): jnp.einsum('trl,trd->ld', grad_scores, query_part, preferred_element_type...  31.1 us
    unnamed x52, local copies, waits for them, and re-layouts  26.1 us
    dot_general x8, matrix products, group_backward(): jnp.einsum('trl,trd->ld', weights_low, grad_part, preferred_element_type=...  24.3 us
    dot_general x8, matrix products, group_forward(): jnp.einsum('trl,ld->trd', weights, value_part, preferred_element_type=jnp...  18.2 us
  transfers between devices with their start and end apart: 19, of which 17 were waited for; matrix products, arithmetic and copies ran while one was open for 14% of the time, Pallas kernels for 0%

commit v1 on v0

--- a/solution.py
+++ b/solution.py
@@ -3,6 +3,7 @@
 import jax.numpy as jnp
 from jax import lax
 from jax.sharding import PartitionSpec as P
+from jax.lax import psum
 
 HD = 128
 WINDOW = 1024
@@ -282,7 +283,7 @@
         value_gradient,
         adapter_up_maps,
     )
-    summed = lax.psum((down_map_gradient, up_map_gradient), ("section", "ctx", "dp"))
+    summed = psum(psum((down_map_gradient, up_map_gradient), ("ctx", "dp")), "section")
     return (handed, summed[0], summed[1])
 
 

time: 642 us -> 678 us (1.056)
  waiting for transfers between devices: 336 us -> 372 us
    psum x1 -> x2, waiting for transfers between devices: 131 us -> 166 us  [the longest x1 151 us: body(): psum((down_map_gradient, up_map_gradient), ('ctx', 'dp'))]
  transfers between devices with their start and end apart: 19 -> 20, of which waited for: 17 -> 18; matrix products, arithmetic and copies ran while one was open for 14% -> 13% of each run, Pallas kernels for 0% -> 0%
where the time goes in v1:
time: 678 us; the launch traced here: 675 us
  waiting for transfers between devices  372 us (55%)
  matrix products  122 us (18%)
  local copies, waits for them, and re-layouts  75.9 us (11%)
  starting transfers between devices  50.2 us (7%)
  other arithmetic  39.1 us (6%)
  between operations  14.6 us (2%)
    ppermute x16, waiting for transfers between devices, passed_along_2(): lax.ppermute(value, axis, [(source, source + steps) for source in range(i...  201 us
    psum x1, waiting for transfers between devices, body(): psum((down_map_gradient, up_map_gradient), ('ctx', 'dp'))  151 us
    ppermute x16, starting transfers between devices, passed_along_2(): lax.ppermute(value, axis, [(source, source + steps) for source in range(i...  50.1 us
    dot_general x16, matrix products, masked_scores(): jnp.einsum('trd,ld->trl', query_part, key_part, preferred_element_type=jn...  41 us
    dot_general x8, matrix products, group_backward(): jnp.einsum('trl,trd->ld', grad_scores, query_part, preferred_element_type...  31 us
    unnamed x52, local copies, waits for them, and re-layouts  26.1 us
    dot_general x8, matrix products, group_backward(): jnp.einsum('trl,trd->ld', weights_low, grad_part, preferred_element_type=...  24.3 us
    dot_general x8, matrix products, group_forward(): jnp.einsum('trl,ld->trd', weights, value_part, preferred_element_type=jnp...  18.2 us
  transfers between devices with their start and end apart: 20, of which 18 were waited for; matrix products, arithmetic and copies ran while one was open for 13% of the time, Pallas kernels for 0%

profile of v1, /device:TPU:0, one launch (start us, length us, event | category | flops | bytes accessed | tf_op | source)
XLA Modules:
  0.0 674.7 jit_solution(8899422376679793045)
XLA Ops:
  17.8 5.7 collective-permute-start
  24.7 3.5 collective-permute-start.4
  28.1 6.9 %collective-permute-done = bf16[256,1024]{0,1:T(8,128)(2,1)} collective-permute-done((bf16[256,1024]{0,1:T(8,128)(2,1)S(1)}, bf16[256,1024]{0,1:T(8,128)(2,1)}, u32[]{:S(2)}, u32[]{:S(2)}) %collective-permute-start) | collective-permute-done | bytes 524320 | tf_op jit(solution)/shard_map/ppermute | solution.py:24
  35.0 5.3 collective-permute-start.1
  46.4 5.2 collective-permute-start.5
  51.6 6.0 collective-permute-done.1
  57.6 5.2 collective-permute-start.2
  68.8 5.2 collective-permute-start.6
  74.1 6.0 collective-permute-done.2
  80.1 4.4 collective-permute-start.3
  87.5 3.9 collective-permute-done.6
  91.3 5.2 collective-permute-start.7
  96.5 6.1 collective-permute-done.3
  109.8 4.4 copy.48
  121.6 46.0 %while.26 = (s32[]{:T(128)}, bf16[8,256,2,128]{3,1,2,0:T(8,128)(2,1)}, f32[8,256,2]{1,2,0:T(2,128)}, bf16[8,256,2,128]{3,1,2,0:T(8,128)(2,1)}, bf16[8,1280,128]{...) while((s32[]{:T(128)}, ...), condition=%wide.region_8.9_spmd.clone, body=%wide.region_5.8_spmd.clone.sunk | while | flops 343145984 | bytes 9469813 | solution.py:246
  167.6 127.1 %while.27 = (s32[]{:T(128)}, f32[8,1280,128]{1,2,0:T(8,128)}, f32[8,1280,128]{1,2,0:T(8,128)}, bf16[8,256,2,128]{3,1,2,0:T(8,128)(2,1)}, bf16[8,1280,128]{2,1,0:...) while((s32[]{:T(128)}, f32[8,1280,128]{1,2,0:T(8,128)}, ...), condition=%wide.region_11.12_spmd.clone, body=%wide.region_9.11_spmd.clone.sunk | while | flops 678395392 | bytes 14472769 | solution.py:252
  168.9 3.3 fusion.128
  174.4 3.9 fusion.130
  184.7 3.3 fusion.128
  190.2 3.9 fusion.130
  200.7 3.3 fusion.128
  206.1 3.9 fusion.130
  212.2 3.1 fusion.131
  216.5 3.3 fusion.128
  222.0 3.9 fusion.130
  228.1 3.1 fusion.131
  232.5 3.3 fusion.128
  237.9 3.9 fusion.130
  248.3 3.3 fusion.128
  253.8 3.9 fusion.130
  259.9 3.0 fusion.131
  264.2 3.3 fusion.128
  269.6 3.9 fusion.130
  280.1 3.3 fusion.128
  285.6 3.9 fusion.130
  301.3 24.9 %collective-permute-done.14 = f32[256,1024]{0,1:T(8,128)S(1)} collective-permute-done((f32[256,1024]{0,1:T(8,128)S(1)}, f32[256,1024]{0,1:T(8,128)S(1)}, u32[]{:S(2)}, u32[]{:S(2)}) %collective-permute-start.14) | collective-permute-done | bytes 1048608 | tf_op jit(solution)/shard_map/ppermute | solution.py:24
  327.6 21.0 %collective-permute-done.10 = f32[256,1024]{0,1:T(8,128)S(1)} collective-permute-done((f32[256,1024]{0,1:T(8,128)S(1)}, f32[256,1024]{0,1:T(8,128)S(1)}, u32[]{:S(2)}, u32[]{:S(2)}) %collective-permute-start.10) | collective-permute-done | bytes 1048608 | tf_op jit(solution)/shard_map/ppermute | solution.py:24
  350.1 21.0 %collective-permute-done.15 = f32[256,1024]{0,1:T(8,128)S(1)} collective-permute-done((f32[256,1024]{0,1:T(8,128)S(1)}, f32[256,1024]{0,1:T(8,128)S(1)}, u32[]{:S(2)}, u32[]{:S(2)}) %collective-permute-start.15) | collective-permute-done | bytes 1048608 | tf_op jit(solution)/shard_map/ppermute | solution.py:24
  372.6 21.0 %collective-permute-done.11 = f32[256,1024]{0,1:T(8,128)S(1)} collective-permute-done((f32[256,1024]{0,1:T(8,128)S(1)}, f32[256,1024]{0,1:T(8,128)S(1)}, u32[]{:S(2)}, u32[]{:S(2)}) %collective-permute-start.11) | collective-permute-done | bytes 1048608 | tf_op jit(solution)/shard_map/ppermute | solution.py:24
  395.0 21.0 %collective-permute-done.16 = f32[256,1024]{0,1:T(8,128)S(1)} collective-permute-done((f32[256,1024]{0,1:T(8,128)S(1)}, f32[256,1024]{0,1:T(8,128)S(1)}, u32[]{:S(2)}, u32[]{:S(2)}) %collective-permute-start.16) | collective-permute-done | bytes 1048608 | tf_op jit(solution)/shard_map/ppermute | solution.py:24
  417.5 21.0 %collective-permute-done.12 = f32[256,1024]{0,1:T(8,128)S(1)} collective-permute-done((f32[256,1024]{0,1:T(8,128)S(1)}, f32[256,1024]{0,1:T(8,128)S(1)}, u32[]{:S(2)}, u32[]{:S(2)}) %collective-permute-start.12) | collective-permute-done | bytes 1048608 | tf_op jit(solution)/shard_map/ppermute | solution.py:24
  440.0 21.0 %collective-permute-done.17 = f32[256,1024]{0,1:T(8,128)S(1)} collective-permute-done((f32[256,1024]{0,1:T(8,128)S(1)}, f32[256,1024]{0,1:T(8,128)S(1)}, u32[]{:S(2)}, u32[]{:S(2)}) %collective-permute-start.17) | collective-permute-done | bytes 1048608 | tf_op jit(solution)/shard_map/ppermute | solution.py:24
  461.7 18.9 %collective-permute-done.13 = f32[256,1024]{0,1:T(8,128)S(1)} collective-permute-done((f32[256,1024]{0,1:T(8,128)S(1)}, f32[256,1024]{0,1:T(8,128)S(1)}, u32[]{:S(2)}, u32[]{:S(2)}) %collective-permute-start.13) | collective-permute-done | bytes 1048608 | tf_op jit(solution)/shard_map/ppermute | solution.py:24
  484.6 151.4 %all-reduce.5.cloned.1.call-done = (f32[5376,2,4,16]{0,3,2,1:T(8,128)}, f32[2,4,16,1024]{3,2,1,0:T(8,128)}) async-done(((f32[5376,2,4,16]{0,3,2,1:T(8,128)}, f32[2,4,16,1024]{3,2,1,0:T(8,128)}), (f32[5376,2,4,16]{0,3,2,1:T(8,128)}, f32[2,4,16,1024]{3,2,1,0:T(8,128)})) %all-reduce.5.cloned.1.call-update) | async-done | bytes 3276816 | tf_op jit(solution)/shard_map/psum | solution.py:286
  636.0 3.3 copy.49
  641.9 4.2 collective-permute-done.8
  646.1 15.1 %all-reduce.7.cloned.1.call-done = (f32[5376,2,4,16]{0,3,2,1:T(8,128)}, f32[2,4,16,1024]{3,2,1,0:T(8,128)}) async-done(((f32[5376,2,4,16]{0,3,2,1:T(8,128)}, f32[2,4,16,1024]{3,2,1,0:T(8,128)}), (f32[5376,2,4,16]{0,3,2,1:T(8,128)}, f32[2,4,16,1024]{3,2,1,0:T(8,128)})) %all-reduce.7.cloned.1.call-update) | async-done | bytes 3276816 | tf_op jit(solution)/shard_map/psum | solution.py:286
  663.4 3.6 copy.116
  (322 shorter events, 172.0 us)
Async XLA Ops:
  7.2 628.8 %all-reduce.5.cloned.1.call-start = ((), (), s32[]{:S(2)}) async-start(), calls=%async_computation | async-start | bytes 6553600 | tf_op jit(solution)/shard_map/psum | solution.py:286
  15.5 8.0 %copy-start.5 = (bf16[2,4,16,1024]{3,2,1,0:T(8,128)(2,1)S(1)}, bf16[2,4,16,1024]{3,2,1,0:T(8,128)(2,1)}, u32[]{:S(2)}) copy-start(bf16[2,4,16,1024]{3,2,1,0:T(8,128)(2,1)} %param.21) | copy-start | bytes 786436
  15.5 8.0 %copy-start.22 = (bf16[1,256,1024]{2,1,0:T(8,128)(2,1)S(1)}, bf16[1,256,1024]{2,1,0:T(8,128)(2,1)}, u32[]{:S(2)}) copy-start(bf16[1,256,1024]{2,1,0:T(8,128)(2,1)} %param.16) | copy-start | bytes 1572868
  17.8 17.2 %collective-permute-start = (bf16[256,1024]{0,1:T(8,128)(2,1)S(1)}, bf16[256,1024]{0,1:T(8,128)(2,1)}, u32[]{:S(2)}, u32[]{:S(2)}) collective-permute-start(bf16[256,1024]{0,1:T(8,128)(2,1)S(1)} %bitcast.243), channel_id=1, source_target_pairs={{0,2},{2,4},{4,6},{6,8},{8,10},{10,12},{12,14},{1,3},{3,5},{5,7},{... | collective-permute-start | bytes 1572872 | tf_op jit(solution)/shard_map/ppermute | solution.py:24
  24.7 21.7 %collective-permute-start.4 = (bf16[256,1024]{1,0:T(8,128)(2,1)}, bf16[256,1024]{1,0:T(8,128)(2,1)}, u32[]{:S(2)}, u32[]{:S(2)}) collective-permute-start(bf16[256,1024]{1,0:T(8,128)(2,1)} %fusion.59), channel_id=1, source_target_pairs={{0,2},{2,4},{4,6},{6,8},{8,10},{10,12},{12,14},{1,3},{3,5},{5,7},{... | collective-permute-start | bytes 1572872 | tf_op jit(solution)/shard_map/ppermute | solution.py:24
  35.0 22.6 %collective-permute-start.1 = (bf16[256,1024]{0,1:T(8,128)(2,1)}, bf16[256,1024]{0,1:T(8,128)(2,1)}, u32[]{:S(2)}, u32[]{:S(2)}) collective-permute-start(bf16[256,1024]{0,1:T(8,128)(2,1)} %collective-permute-done), channel_id=1, source_target_pairs={{0,2},{2,4},{4,6},{6,8},{8,10},{10,12},{12,14},{1,3},{3,5},{5,7},{... | collective-permute-start | bytes 1572872 | tf_op jit(solution)/shard_map/ppermute | solution.py:24
  42.6 125.1 %collective-permute-start.9 = (bf16[1,256,2048]{1,2,0:T(8,128)(2,1)}, bf16[1,256,2048]{1,2,0:T(8,128)(2,1)}, u32[]{:S(2)}, u32[]{:S(2)}) collective-permute-start(bf16[1,256,2048]{1,2,0:T(8,128)(2,1)} %copy.50), channel_id=1, source_target_pairs={{0,16},{16,0},{1,17},{17,1},{2,18},{18,2},{3,19},{19,3},{4,20},{20... | collective-permute-start | bytes 3145736 | tf_op jit(solution)/shard_map/ppermute | solution.py:18
  46.4 22.5 %collective-permute-start.5 = (bf16[256,1024]{1,0:T(8,128)(2,1)}, bf16[256,1024]{1,0:T(8,128)(2,1)}, u32[]{:S(2)}, u32[]{:S(2)}) collective-permute-start(bf16[256,1024]{1,0:T(8,128)(2,1)} %collective-permute-done.4), channel_id=1, source_target_pairs={{0,2},{2,4},{4,6},{6,8},{8,10},{10,12},{12,14},{1,3},{3,5},{5,7},{... | collective-permute-start | bytes 1572872 | tf_op jit(solution)/shard_map/ppermute | solution.py:24
  57.6 22.5 %collective-permute-start.2 = (bf16[256,1024]{0,1:T(8,128)(2,1)}, bf16[256,1024]{0,1:T(8,128)(2,1)}, u32[]{:S(2)}, u32[]{:S(2)}) collective-permute-start(bf16[256,1024]{0,1:T(8,128)(2,1)} %collective-permute-done.1), channel_id=1, source_target_pairs={{0,2},{2,4},{4,6},{6,8},{8,10},{10,12},{12,14},{1,3},{3,5},{5,7},{... | collective-permute-start | bytes 1572872 | tf_op jit(solution)/shard_map/ppermute | solution.py:24
  66.9 17.5 %copy-start.1 = (f32[256,64]{1,0:T(8,128)S(1)}, f32[256,64]{1,0:T(8,128)}, u32[]{:S(2)}) copy-start(f32[256,64]{1,0:T(8,128)} %copy.41) | copy-start | bytes 196612
  67.0 17.5 %copy-start.2 = (f32[256,64]{1,0:T(8,128)S(1)}, f32[256,64]{1,0:T(8,128)}, u32[]{:S(2)}) copy-start(f32[256,64]{1,0:T(8,128)} %copy.43) | copy-start | bytes 196612
  68.8 22.5 %collective-permute-start.6 = (bf16[256,1024]{1,0:T(8,128)(2,1)}, bf16[256,1024]{1,0:T(8,128)(2,1)}, u32[]{:S(2)}, u32[]{:S(2)}) collective-permute-start(bf16[256,1024]{1,0:T(8,128)(2,1)} %collective-permute-done.5), channel_id=1, source_target_pairs={{0,2},{2,4},{4,6},{6,8},{8,10},{10,12},{12,14},{1,3},{3,5},{5,7},{... | collective-permute-start | bytes 1572872 | tf_op jit(solution)/shard_map/ppermute | solution.py:24
  80.1 22.5 %collective-permute-start.3 = (bf16[256,1024]{0,1:T(8,128)(2,1)}, bf16[256,1024]{0,1:T(8,128)(2,1)S(1)}, u32[]{:S(2)}, u32[]{:S(2)}) collective-permute-start(bf16[256,1024]{0,1:T(8,128)(2,1)} %collective-permute-done.2), channel_id=1, source_target_pairs={{0,2},{2,4},{4,6},{6,8},{8,10},{10,12},{12,14},{1,3},{3,5},{5,7},{... | collective-permute-start | bytes 1572872 | tf_op jit(solution)/shard_map/ppermute | solution.py:24
  91.3 22.9 %collective-permute-start.7 = (bf16[256,1024]{1,0:T(8,128)(2,1)}, bf16[256,1024]{1,0:T(8,128)(2,1)}, u32[]{:S(2)}, u32[]{:S(2)}) collective-permute-start(bf16[256,1024]{1,0:T(8,128)(2,1)} %collective-permute-done.6), channel_id=1, source_target_pairs={{0,2},{2,4},{4,6},{6,8},{8,10},{10,12},{12,14},{1,3},{3,5},{5,7},{... | collective-permute-start | bytes 1572872 | tf_op jit(solution)/shard_map/ppermute | solution.py:24
  167.6 4.6 copy-start.9
  167.6 4.6 copy-start.13
  167.7 4.6 copy-start.17
  183.5 4.6 copy-start.9
  183.5 4.6 copy-start.13
  199.4 4.6 copy-start.9
  199.4 4.6 copy-start.13
  199.4 4.6 copy-start.17
  215.3 4.6 copy-start.9
  215.3 4.6 copy-start.13
  231.2 4.6 copy-start.9
  231.2 4.6 copy-start.13
  231.3 4.6 copy-start.17
  247.1 4.6 copy-start.9
  247.1 4.6 copy-start.13
  247.1 4.6 copy-start.17
  262.9 4.6 copy-start.9
  263.0 4.6 copy-start.13
  263.0 4.6 copy-start.17
  278.8 4.6 copy-start.9
  278.8 4.6 copy-start.13
  278.8 4.6 copy-start.17
  297.8 28.4 %collective-permute-start.14 = (f32[256,1024]{0,1:T(8,128)S(1)}, f32[256,1024]{0,1:T(8,128)S(1)}, u32[]{:S(2)}, u32[]{:S(2)}) collective-permute-start(f32[256,1024]{0,1:T(8,128)S(1)} %bitcast.238), channel_id=1, source_target_pairs={{2,0},{4,2},{6,4},{8,6},{10,8},{12,10},{14,12},{3,1},{5,3},{7,5},{... | collective-permute-start | bytes 3145736 | tf_op jit(solution)/shard_map/ppermute | solution.py:24
  300.0 48.7 %collective-permute-start.10 = (f32[256,1024]{0,1:T(8,128)S(1)}, f32[256,1024]{0,1:T(8,128)S(1)}, u32[]{:S(2)}, u32[]{:S(2)}) collective-permute-start(f32[256,1024]{0,1:T(8,128)S(1)} %bitcast.239), channel_id=1, source_target_pairs={{2,0},{4,2},{6,4},{8,6},{10,8},{12,10},{14,12},{3,1},{5,3},{7,5},{... | collective-permute-start | bytes 3145736 | tf_op jit(solution)/shard_map/ppermute | solution.py:24
  326.3 44.8 %collective-permute-start.15 = (f32[256,1024]{0,1:T(8,128)S(1)}, f32[256,1024]{0,1:T(8,128)S(1)}, u32[]{:S(2)}, u32[]{:S(2)}) collective-permute-start(f32[256,1024]{0,1:T(8,128)S(1)} %bitcast_add_fusion.3), channel_id=1, source_target_pairs={{2,0},{4,2},{6,4},{8,6},{10,8},{12,10},{14,12},{3,1},{5,3},{7,5},{... | collective-permute-start | bytes 3145736 | tf_op jit(solution)/shard_map/ppermute | solution.py:24
  348.8 44.8 %collective-permute-start.11 = (f32[256,1024]{0,1:T(8,128)S(1)}, f32[256,1024]{0,1:T(8,128)S(1)}, u32[]{:S(2)}, u32[]{:S(2)}) collective-permute-start(f32[256,1024]{0,1:T(8,128)S(1)} %bitcast_add_fusion.7), channel_id=1, source_target_pairs={{2,0},{4,2},{6,4},{8,6},{10,8},{12,10},{14,12},{3,1},{5,3},{7,5},{... | collective-permute-start | bytes 3145736 | tf_op jit(solution)/shard_map/ppermute | solution.py:24
  371.3 44.8 %collective-permute-start.16 = (f32[256,1024]{0,1:T(8,128)S(1)}, f32[256,1024]{0,1:T(8,128)S(1)}, u32[]{:S(2)}, u32[]{:S(2)}) collective-permute-start(f32[256,1024]{0,1:T(8,128)S(1)} %bitcast_add_fusion.2), channel_id=1, source_target_pairs={{2,0},{4,2},{6,4},{8,6},{10,8},{12,10},{14,12},{3,1},{5,3},{7,5},{... | collective-permute-start | bytes 3145736 | tf_op jit(solution)/shard_map/ppermute | solution.py:24
  393.7 44.8 %collective-permute-start.12 = (f32[256,1024]{0,1:T(8,128)S(1)}, f32[256,1024]{0,1:T(8,128)S(1)}, u32[]{:S(2)}, u32[]{:S(2)}) collective-permute-start(f32[256,1024]{0,1:T(8,128)S(1)} %bitcast_add_fusion.6), channel_id=1, source_target_pairs={{2,0},{4,2},{6,4},{8,6},{10,8},{12,10},{14,12},{3,1},{5,3},{7,5},{... | collective-permute-start | bytes 3145736 | tf_op jit(solution)/shard_map/ppermute | solution.py:24
  416.1 23.9 %copy-start.6 = (bf16[2,4,16,1024]{3,2,1,0:T(8,128)(2,1)S(1)}, bf16[2,4,16,1024]{3,2,1,0:T(8,128)(2,1)}, u32[]{:S(2)}) copy-start(bf16[2,4,16,1024]{3,2,1,0:T(8,128)(2,1)} %param.21) | copy-start | bytes 786436
  416.2 44.8 %collective-permute-start.17 = (f32[256,1024]{0,1:T(8,128)S(1)}, f32[256,1024]{0,1:T(8,128)S(1)}, u32[]{:S(2)}, u32[]{:S(2)}) collective-permute-start(f32[256,1024]{0,1:T(8,128)S(1)} %bitcast_add_fusion.1), channel_id=1, source_target_pairs={{2,0},{4,2},{6,4},{8,6},{10,8},{12,10},{14,12},{3,1},{5,3},{7,5},{... | collective-permute-start | bytes 3145736 | tf_op jit(solution)/shard_map/ppermute | solution.py:24
  438.7 42.0 %collective-permute-start.13 = (f32[256,1024]{0,1:T(8,128)S(1)}, f32[256,1024]{0,1:T(8,128)S(1)}, u32[]{:S(2)}, u32[]{:S(2)}) collective-permute-start(f32[256,1024]{0,1:T(8,128)S(1)} %bitcast_add_fusion.5), channel_id=1, source_target_pairs={{2,0},{4,2},{6,4},{8,6},{10,8},{12,10},{14,12},{3,1},{5,3},{7,5},{... | collective-permute-start | bytes 3145736 | tf_op jit(solution)/shard_map/ppermute | solution.py:24
  461.2 19.6 %copy-start.7 = (f32[256,64]{0,1:T(8,128)S(1)}, f32[256,64]{0,1:T(8,128)}, u32[]{:S(2)}) copy-start(f32[256,64]{0,1:T(8,128)} %get-tuple-element.292) | copy-start | bytes 196612
  484.5 176.6 %all-reduce.7.cloned.1.call-start = ((), (), s32[]{:S(2)}) async-start(), calls=%async_computation.1 | async-start | bytes 6553600 | tf_op jit(solution)/shard_map/psum | solution.py:286
  641.9 4.2 collective-permute-start.8
  (39 other events, 116.2 us)
Sparse Core Ops, SparseCore 0:
  484.6 151.2 all-reduce.4
  638.3 22.7 all-reduce.6
